TPU v7x, 32 devices: a whole 2x2x4 slice. The times are simulated.
32 devices in a mesh: gx: 8 (over y, x, core), gy: 4 (over z).
Axes of the slice: x: 2, y: 2, z: 4, core: 2. Of those that a mesh axis runs over, the one named last changes fastest.
Arguments:
- eastward: float32 [64, 512, 128], P('gx', 'gy'), may hold values from -6 to 6
- northward: float32 [64, 512, 128], P('gx', 'gy'), may hold values from -6 to 6
- vertical: float32 [64, 512, 128], P('gx', 'gy'), may hold values from -6 to 6
- pressure: float32 [64, 512, 128], P('gx', 'gy'), may hold values from -6 to 6
- theta: float32 [64, 512, 128], P('gx', 'gy'), may hold values from -6 to 6
- humidity: float32 [64, 512, 128], P('gx', 'gy'), may hold values from 0.95 to 1.07
- sound_speed: float32 [128], replicated, may hold values from 0.25 to 1
- radius_sq: float32 [64, 8, 64, 512], P(None, None, 'gx', 'gy'), may hold values from 0.25 to 4
- multiplicity: bfloat16 [64, 8, 64, 512], P(None, None, 'gx', 'gy'), may hold values from 0.5 to 2
- droplet_count: int32 [8, 64, 512], P(None, 'gx', 'gy'), may hold values from 0 to 64
Outputs:
- eastward_out: float32 [64, 512, 128], P('gx', 'gy')
- northward_out: float32 [64, 512, 128], P('gx', 'gy')
- vertical_out: float32 [64, 512, 128], P('gx', 'gy')
- pressure_out: float32 [64, 512, 128], P('gx', 'gy')
- theta_out: float32 [64, 512, 128], P('gx', 'gy')
- humidity_out: float32 [64, 512, 128], P('gx', 'gy')
- radius_out: float32 [64, 8, 64, 512], P(None, None, 'gx', 'gy')
- saturation_profile: float32 [128], replicated
All inputs are finite; a program needn't handle non-finite values.
Results may differ from a plain program's by a relative error of at most 0.0003.
Values sent between devices are 32-bit elements; how exact they have to be, the bound alone decides.
No kernel may reach another device: no remote copies, remote signals or barrier semaphores. Data moves between devices by JAX's collectives and lax.ppermute only.
A program may use at most 64 MiB of HBM per device.

v0:
```python
import jax
import jax.numpy as jnp
from jax import lax
from jax.sharding import PartitionSpec as P

SUB = 3
TIME_STEP = 1.0
BUOYANCY = 0.5
VAPOUR_SLOPE = 0.01
GROWTH_RATE = 25.0
RADIUS_FLOOR = 0.0625
MASS_FACTOR = 0.0004
LATENT_HEAT = 200.0


def padded_2(value, sides, width):
    for axis, dim in sides:
        count, length = (lax.axis_size(axis), value.shape[dim])
        up = [(i, (i + 1) % count) for i in range(count)]
        down = [(j, i) for i, j in up]
        last = lax.slice_in_dim(value, length - width, length, axis=dim)
        initial = lax.slice_in_dim(value, 0, width, axis=dim)
        before = lax.ppermute(last, axis, up)
        after = lax.ppermute(initial, axis, down)
        value = jnp.concatenate([before, value, after], axis=dim)
    return value


def column_tables(sound_speed):
    levels = sound_speed.shape[0]
    rows = lax.broadcasted_iota(jnp.int32, (levels, levels), 0)
    cols = lax.broadcasted_iota(jnp.int32, (levels, levels), 1)
    inside = rows < levels - 1
    gradient = jnp.where(inside & (cols == rows + 1), 1.0, 0.0) - jnp.where(
        inside & (cols == rows), 1.0, 0.0
    )
    gradient = gradient.astype(jnp.float32)
    scaled = gradient * sound_speed[None, :]
    product = jnp.dot(
        scaled, gradient.T, precision=lax.Precision.HIGHEST, preferred_element_type=jnp.float32
    )
    matrix = jnp.eye(levels, dtype=jnp.float32) + TIME_STEP * TIME_STEP * product
    factor = jnp.linalg.cholesky(matrix)
    identity = jnp.eye(levels, dtype=jnp.float32)
    halfway = lax.linalg.triangular_solve(factor, identity, left_side=True, lower=True)
    inverse = lax.linalg.triangular_solve(
        factor, halfway, left_side=True, lower=True, transpose_a=True
    )
    lifted = TIME_STEP * jnp.dot(
        gradient.T, inverse, precision=lax.Precision.HIGHEST, preferred_element_type=jnp.float32
    )
    return (inverse, lifted, gradient)


def column_update(pressure, vertical, heat, divergence, sound_speed, tables):
    inverse, lifted, gradient = tables
    levels = pressure.shape[-1]
    interior = (lax.broadcasted_iota(jnp.int32, (levels,), 0) < levels - 1).astype(jnp.float32)
    explicit = pressure - TIME_STEP * sound_speed * divergence
    forcing = (interior * (vertical + TIME_STEP * BUOYANCY * heat)).reshape(-1, levels)
    flat_explicit = explicit.reshape(-1, levels)
    solved = jnp.dot(
        forcing, inverse, precision=lax.Precision.HIGHEST, preferred_element_type=jnp.float32
    )
    solved = solved - jnp.dot(
        flat_explicit, lifted, precision=lax.Precision.HIGHEST, preferred_element_type=jnp.float32
    )
    stepped = jnp.dot(
        solved, gradient, precision=lax.Precision.HIGHEST, preferred_element_type=jnp.float32
    )
    new_pressure = flat_explicit + TIME_STEP * sound_speed * stepped
    return (new_pressure.reshape(explicit.shape), solved.reshape(explicit.shape))


def horizontal_velocity(eastward, northward, padded):
    grad_east = (padded[2:, 1:-1] - padded[:-2, 1:-1]) * 0.5
    grad_north = (padded[1:-1, 2:] - padded[1:-1, :-2]) * 0.5
    return (eastward - TIME_STEP * grad_east, northward - TIME_STEP * grad_north)


def horizontal_spread(east_padded, north_padded):
    return (
        east_padded[2:, 1:-1]
        - east_padded[:-2, 1:-1]
        + north_padded[1:-1, 2:]
        - north_padded[1:-1, :-2]
    ) * 0.5


def condense(theta, humidity, radius_sq, multiplicity, droplet_count):
    levels = theta.shape[2]
    layers = radius_sq.shape[1]
    lowest = levels // 4
    sat = humidity * jnp.exp(-VAPOUR_SLOPE * theta) - 1.0
    cloud = jnp.transpose(sat[:, :, lowest : lowest + layers], (2, 0, 1))
    grown = jnp.maximum(radius_sq + GROWTH_RATE * cloud[None], RADIUS_FLOOR)
    live = lax.broadcasted_iota(jnp.int32, radius_sq.shape, 0) < droplet_count[None]
    mass = multiplicity.astype(jnp.float32) * (
        grown * jnp.sqrt(grown) - radius_sq * jnp.sqrt(radius_sq)
    )
    change = MASS_FACTOR * jnp.sum(jnp.where(live, mass, 0.0), axis=0)
    added = jnp.pad(
        jnp.transpose(change, (1, 2, 0)), ((0, 0), (0, 0), (lowest, levels - lowest - layers))
    )
    humidity_out = humidity - added
    theta_out = theta + LATENT_HEAT * added
    radius_out = jnp.where(live, grown, 0.0)
    percent = 100.0 * (humidity_out * jnp.exp(-VAPOUR_SLOPE * theta_out) - 1.0)
    return (humidity_out, theta_out, radius_out, percent)


def level_means(percent, theta_out, columns):
    totals = lax.psum(
        (jnp.sum(percent, axis=(0, 1)), jnp.sum(theta_out, axis=(0, 1))), ("gx", "gy")
    )
    return (totals[0] / columns, totals[1] / columns)


def local(
    eastward,
    northward,
    vertical,
    pressure,
    theta,
    humidity,
    sound_speed,
    radius_sq,
    multiplicity,
    droplet_count,
):
    humidity_out, theta_out, radius_out, percent = condense(
        theta, humidity, radius_sq, multiplicity, droplet_count
    )
    columns = float(theta.shape[0] * theta.shape[1] * lax.axis_size("gx") * lax.axis_size("gy"))
    tables = column_tables(sound_speed)
    saturation_profile, theta_mean = level_means(percent, theta_out, columns)
    heat = theta_out - theta_mean
    margin = 2 * SUB
    eastward, northward, vertical, pressure, heating = (
        padded_2(eastward, (("gx", 0), ("gy", 1)), margin),
        padded_2(northward, (("gx", 0), ("gy", 1)), margin),
        padded_2(vertical, (("gx", 0), ("gy", 1)), margin),
        padded_2(pressure, (("gx", 0), ("gy", 1)), margin),
        padded_2(heat, (("gx", 0), ("gy", 1)), margin),
    )
    for substep in range(SUB):
        east_new, north_new = horizontal_velocity(
            eastward[1:-1, 1:-1], northward[1:-1, 1:-1], pressure
        )
        spread = horizontal_spread(east_new, north_new)
        heating = heating[2:-2, 2:-2]
        pressure, vertical = column_update(
            pressure[2:-2, 2:-2], vertical[2:-2, 2:-2], heating, spread, sound_speed, tables
        )
        eastward, northward = (east_new[1:-1, 1:-1], north_new[1:-1, 1:-1])
    return (
        eastward,
        northward,
        vertical,
        pressure,
        theta_out,
        humidity_out,
        radius_out,
        saturation_profile,
    )


def solution(mesh):
    return jax.shard_map(
        local,
        mesh=mesh,
        in_specs=(
            P("gx", "gy", None),
            P("gx", "gy", None),
            P("gx", "gy", None),
            P("gx", "gy", None),
            P("gx", "gy", None),
            P("gx", "gy", None),
            P(),
            P(None, None, "gx", "gy"),
            P(None, None, "gx", "gy"),
            P(None, "gx", "gy"),
        ),
        out_specs=(
            P("gx", "gy", None),
            P("gx", "gy", None),
            P("gx", "gy", None),
            P("gx", "gy", None),
            P("gx", "gy", None),
            P("gx", "gy", None),
            P(None, None, "gx", "gy"),
            P(),
        ),
        check_vma=False,
    )
```

profile of v0, /device:TPU:0, one launch (start us, length us, event | category | flops | bytes accessed | tf_op | source)
XLA Modules:
  0.0 179.3 jit_solution(16261416911662587209)
XLA Ops:
  0.7 2.1 %fusion.102 = (f32[6,128,128]{2,1,0:T(8,128)}, f32[6,128,128]{2,1,0:T(8,128)}) fusion(f32[8,128,128]{2,1,0:T(8,128)} %param.13), kind=kLoop, calls=%fused_computation.159 | loop fusion | bytes 1572864 | tf_op jit(solution)/shard_map/slice | solution.py:22
  3.3 2.9 %collective-permute-start.5 = (f32[6,128,128]{2,1,0:T(8,128)}, f32[6,128,128]{2,1,0:T(8,128)}, u32[]{:S(2)}, u32[]{:S(2)}) collective-permute-start(f32[6,128,128]{2,1,0:T(8,128)} %get-tuple-element.67), channel_id=1, source_target_pairs={{4,0},{8,4},{12,8},{16,12},{20,16},{24,20},{28,24},{0,28},{5,1},{9... | collective-permute-start | bytes 1179656 | tf_op jit(solution)/shard_map/ppermute | solution.py:24
  7.2 2.6 %collective-permute-start.1 = (f32[6,128,128]{2,1,0:T(8,128)}, f32[6,128,128]{2,1,0:T(8,128)}, u32[]{:S(2)}, u32[]{:S(2)}) collective-permute-start(f32[6,128,128]{2,1,0:T(8,128)} %get-tuple-element.63), channel_id=1, source_target_pairs={{4,0},{8,4},{12,8},{16,12},{20,16},{24,20},{28,24},{0,28},{5,1},{9... | collective-permute-start | bytes 1179656 | tf_op jit(solution)/shard_map/ppermute | solution.py:24
  11.5 4.9 %fusion.6 = (f32[64,8,8,128]{3,2,1,0:T(8,128)}, f32[8,8,128]{2,1,0:T(8,128)S(1)}) fusion(f32[64,8,8,128]{3,2,1,0:T(8,128)} %param.17, f32[8,8,128]{2,1,0:T(8,128)S(1)} %fusion.58, s32[8,8,128]{2,1,0:T(8,128)S(1)} %copy-done.26, bf16[64,8,8,128]{3,2,1,0:T(8,128)(2,1)} %param.18), kind=kLoop, calls=%fused_computation.13 | loop fusion | flops 5758976 | bytes 5341184 | tf_op jit(solution)/shard_map/jit(_where)/select_n | solution.py:107
  17.4 44.2 %all-reduce.1 = (f32[128]{0:T(128)S(1)}, f32[128]{0:T(128)S(1)}) all-reduce(f32[128]{0:T(128)S(1)} %get-tuple-element.33, f32[128]{0:T(128)S(1)} %get-tuple-element.32), channel_id=1, replica_groups=mesh['gx'=8,'gy'=4] {'gx','gy'}, use_global_device_ids=true, to_apply=%region_2.3 | all-reduce | flops 256 | bytes 2048 | tf_op jit(solution)/shard_map/psum | solution.py:113
  63.8 11.7 %cholesky.17 = f32[128,128]{1,0:T(8,128)S(1)} custom-call(f32[128,128]{1,0:T(8,128)S(1)} %fusion.42), custom_call_target="Cholesky" | custom-call | tf_op jit(solution)/shard_map/jit(cholesky)/cholesky | solution.py:43
  76.9 9.8 %custom-call.8 = f32[1,128,128]{1,2,0:T(8,128)S(1)} custom-call(f32[1,128,128]{2,1,0:T(8,128)S(1)} %fusion.36), custom_call_target="InvertDiagBlocksLowerTriangular" | custom-call | tf_op jit(solution)/shard_map/triangular_solve | solution.py:46
  94.3 2.7 %collective-permute-start.9 = (f32[6,128,128]{2,1,0:T(8,128)}, f32[6,128,128]{2,1,0:T(8,128)}, u32[]{:S(2)}, u32[]{:S(2)}) collective-permute-start(f32[6,128,128]{2,1,0:T(8,128)} %get-tuple-element.65), channel_id=1, source_target_pairs={{4,0},{8,4},{12,8},{16,12},{20,16},{24,20},{28,24},{0,28},{5,1},{9... | collective-permute-start | bytes 1179656 | tf_op jit(solution)/shard_map/ppermute | solution.py:24
  98.1 4.5 %collective-permute-done.17 = f32[6,128,128]{1,0,2:T(8,128)S(1)} collective-permute-done((f32[6,128,128]{1,0,2:T(8,128)S(1)}, f32[6,128,128]{1,0,2:T(8,128)S(1)}, u32[]{:S(2)}, u32[]{:S(2)}) %collective-permute-start.17) | collective-permute-done | bytes 393248 | tf_op jit(solution)/shard_map/ppermute | solution.py:24
  102.5 2.8 %collective-permute-start.13 = (f32[6,128,128]{2,0,1:T(8,128)}, f32[6,128,128]{2,0,1:T(8,128)}, u32[]{:S(2)}, u32[]{:S(2)}) collective-permute-start(f32[6,128,128]{2,0,1:T(8,128)} %get-tuple-element.60), channel_id=1, source_target_pairs={{4,0},{8,4},{12,8},{16,12},{20,16},{24,20},{28,24},{0,28},{5,1},{9... | collective-permute-start | bytes 1179656 | tf_op jit(solution)/shard_map/ppermute | solution.py:24
  105.3 3.0 %collective-permute-done.16 = f32[6,128,128]{1,0,2:T(8,128)S(1)} collective-permute-done((f32[6,128,128]{1,0,2:T(8,128)S(1)}, f32[6,128,128]{1,0,2:T(8,128)S(1)}, u32[]{:S(2)}, u32[]{:S(2)}) %collective-permute-start.16) | collective-permute-done | bytes 393248 | tf_op jit(solution)/shard_map/ppermute | solution.py:23
  111.2 2.1 %fusion.94 = (f32[20,6,128]{1,0,2:T(8,128)}, f32[20,6,128]{1,0,2:T(8,128)}) fusion(f32[20,128,128]{1,0,2:T(8,128)S(1)} %pad_maximum_fusion.1), kind=kLoop, calls=%fused_computation.151 | loop fusion | bytes 245760 | tf_op jit(solution)/shard_map/slice | solution.py:21
  120.8 3.4 %collective-permute-start.3 = (f32[20,6,128]{2,1,0:T(8,128)S(1)}, f32[20,6,128]{2,1,0:T(8,128)S(1)}, u32[]{:S(2)}, u32[]{:S(2)}) collective-permute-start(f32[20,6,128]{2,1,0:T(8,128)S(1)} %get-tuple-element.47), channel_id=1, source_target_pairs={{1,0},{2,1},{3,2},{0,3},{5,4},{6,5},{7,6},{4,7},{9,8},{10,9},{11,1... | collective-permute-start | bytes 184328 | tf_op jit(solution)/shard_map/ppermute | solution.py:24
  127.0 2.0 %collective-permute-start.18 = (f32[20,6,128]{2,0,1:T(8,128)S(1)}, f32[20,6,128]{2,0,1:T(8,128)S(1)}, u32[]{:S(2)}, u32[]{:S(2)}) collective-permute-start(f32[20,6,128]{2,0,1:T(8,128)S(1)} %copy.55), channel_id=1, source_target_pairs={{0,1},{1,2},{2,3},{3,0},{4,5},{5,6},{6,7},{7,4},{8,9},{9,10},{10,1... | collective-permute-start | bytes 184328 | tf_op jit(solution)/shard_map/ppermute | solution.py:23
  134.9 2.1 %collective-permute-start.15 = (f32[20,6,128]{2,0,1:T(8,128)S(1)}, f32[20,6,128]{2,0,1:T(8,128)S(1)}, u32[]{:S(2)}, u32[]{:S(2)}) collective-permute-start(f32[20,6,128]{2,0,1:T(8,128)S(1)} %get-tuple-element.41), channel_id=1, source_target_pairs={{1,0},{2,1},{3,2},{0,3},{5,4},{6,5},{7,6},{4,7},{9,8},{10,9},{11,1... | collective-permute-start | bytes 184328 | tf_op jit(solution)/shard_map/ppermute | solution.py:24
  137.3 2.4 %collective-permute-done.15 = f32[20,6,128]{2,0,1:T(8,128)S(1)} collective-permute-done((f32[20,6,128]{2,0,1:T(8,128)S(1)}, f32[20,6,128]{2,0,1:T(8,128)S(1)}, u32[]{:S(2)}, u32[]{:S(2)}) %collective-permute-start.15) | collective-permute-done | bytes 61472 | tf_op jit(solution)/shard_map/ppermute | solution.py:24
  139.7 4.5 %collective-permute-done.14 = f32[20,6,128]{2,0,1:T(8,128)S(1)} collective-permute-done((f32[20,6,128]{2,0,1:T(8,128)S(1)}, f32[20,6,128]{2,0,1:T(8,128)S(1)}, u32[]{:S(2)}, u32[]{:S(2)}) %collective-permute-start.14) | collective-permute-done | bytes 61472 | tf_op jit(solution)/shard_map/ppermute | solution.py:23
  145.6 2.1 %collective-permute-start.10 = (f32[20,6,128]{2,1,0:T(8,128)S(1)}, f32[20,6,128]{2,1,0:T(8,128)S(1)}, u32[]{:S(2)}, u32[]{:S(2)}) collective-permute-start(f32[20,6,128]{2,1,0:T(8,128)S(1)} %get-tuple-element.48), channel_id=1, source_target_pairs={{0,1},{1,2},{2,3},{3,0},{4,5},{5,6},{6,7},{7,4},{8,9},{9,10},{10,1... | collective-permute-start | bytes 184328 | tf_op jit(solution)/shard_map/ppermute | solution.py:23
  149.1 2.8 %collective-permute-done.10 = f32[20,6,128]{2,1,0:T(8,128)S(1)} collective-permute-done((f32[20,6,128]{2,1,0:T(8,128)S(1)}, f32[20,6,128]{2,1,0:T(8,128)S(1)}, u32[]{:S(2)}, u32[]{:S(2)}) %collective-permute-start.10) | collective-permute-done | bytes 61472 | tf_op jit(solution)/shard_map/ppermute | solution.py:23
  157.0 2.1 %reshape.77 = f32[1584,128]{1,0:T(8,128)} reshape(f32[12,132,128]{2,1,0:T(8,128)} %fusion.23) | data formatting | bytes 1622016 | tf_op jit(solution)/shard_map/reshape | solution.py:61
  159.1 2.3 %fusion.21 = f32[12,132,128]{2,1,0:T(8,128)} fusion(f32[20,140,128]{2,1,0:T(8,128)} %copy-done.2, f32[16,136,128]{2,1,0:T(8,128)S(1)} %bitcast.50, f32[128]{0:T(128)S(1)} %fusion.81), kind=kLoop, calls=%fused_computation.50 | loop fusion | flops 608256 | bytes 2433536 | tf_op jit(solution)/shard_map/mul | solution.py:60
  161.3 2.2 %reshape.79 = f32[1584,128]{1,0:T(8,128)} reshape(f32[12,132,128]{2,1,0:T(8,128)} %fusion.21) | data formatting | bytes 1622016 | tf_op jit(solution)/shard_map/reshape | solution.py:60
  163.5 1.9 %fusion.104 = f32[1584,128]{1,0:T(8,128)S(1)} fusion(f32[1584,128]{1,0:T(8,128)} %reshape.79, f32[128,128]{1,0:T(8,128)S(1)} %fusion.37), kind=kOutput, calls=%fused_computation.161 | convolution fusion | flops 311427072 | bytes 1687552 | tf_op jit(solution)/shard_map/dot_general | solution.py:62
  169.0 2.1 %reshape.81 = f32[12,132,128]{2,1,0:T(8,128)} reshape(f32[1584,128]{1,0:T(8,128)} %copy-done.5) | data formatting | bytes 1622016 | tf_op jit(solution)/shard_map/reshape | solution.py:72
  (170 shorter events, 54.8 us)
Async XLA Ops:
  2.8 88.2 %collective-permute-start.4 = (f32[6,128,128]{2,1,0:T(8,128)}, f32[6,128,128]{2,1,0:T(8,128)}, u32[]{:S(2)}, u32[]{:S(2)}) collective-permute-start(f32[6,128,128]{2,1,0:T(8,128)} %get-tuple-element.68), channel_id=1, source_target_pairs={{0,4},{4,8},{8,12},{12,16},{16,20},{20,24},{24,28},{28,0},{1,5},{5... | collective-permute-start | bytes 1179656 | tf_op jit(solution)/shard_map/ppermute | solution.py:23
  3.3 91.0 %collective-permute-start.5 = (f32[6,128,128]{2,1,0:T(8,128)}, f32[6,128,128]{2,1,0:T(8,128)}, u32[]{:S(2)}, u32[]{:S(2)}) collective-permute-start(f32[6,128,128]{2,1,0:T(8,128)} %get-tuple-element.67), channel_id=1, source_target_pairs={{4,0},{8,4},{12,8},{16,12},{20,16},{24,20},{28,24},{0,28},{5,1},{9... | collective-permute-start | bytes 1179656 | tf_op jit(solution)/shard_map/ppermute | solution.py:24
  7.2 86.0 %collective-permute-start = (f32[6,128,128]{2,1,0:T(8,128)}, f32[6,128,128]{2,1,0:T(8,128)}, u32[]{:S(2)}, u32[]{:S(2)}) collective-permute-start(f32[6,128,128]{2,1,0:T(8,128)} %get-tuple-element.64), channel_id=1, source_target_pairs={{0,4},{4,8},{8,12},{12,16},{16,20},{20,24},{24,28},{28,0},{1,5},{5... | collective-permute-start | bytes 1179656 | tf_op jit(solution)/shard_map/ppermute | solution.py:23
  7.2 106.2 %collective-permute-start.1 = (f32[6,128,128]{2,1,0:T(8,128)}, f32[6,128,128]{2,1,0:T(8,128)}, u32[]{:S(2)}, u32[]{:S(2)}) collective-permute-start(f32[6,128,128]{2,1,0:T(8,128)} %get-tuple-element.63), channel_id=1, source_target_pairs={{4,0},{8,4},{12,8},{16,12},{20,16},{24,20},{28,24},{0,28},{5,1},{9... | collective-permute-start | bytes 1179656 | tf_op jit(solution)/shard_map/ppermute | solution.py:24
  10.8 97.8 %collective-permute-start.8 = (f32[6,128,128]{2,1,0:T(8,128)}, f32[6,128,128]{2,1,0:T(8,128)}, u32[]{:S(2)}, u32[]{:S(2)}) collective-permute-start(f32[6,128,128]{2,1,0:T(8,128)} %get-tuple-element.66), channel_id=1, source_target_pairs={{0,4},{4,8},{8,12},{12,16},{16,20},{20,24},{24,28},{28,0},{1,5},{5... | collective-permute-start | bytes 1179656 | tf_op jit(solution)/shard_map/ppermute | solution.py:23
  10.8 155.5 %copy-start.28 = (s32[128]{0:T(128)}, s32[128]{0:T(128)S(1)}, u32[]{:S(2)}) copy-start(s32[128]{0:T(128)S(1)} %iota_add_fusion) | copy-start | bytes 1540
  10.8 155.5 %copy-start.30 = (pred[128]{0:T(512)(128)(4,1)}, pred[128]{0:T(512)(128)(4,1)S(1)}, u32[]{:S(2)}) copy-start(pred[128]{0:T(512)(128)(4,1)S(1)} %iota_compare_fusion.6) | copy-start | bytes 388
  87.5 77.9 %copy-start.19 = (f32[128,128]{1,0:T(8,128)}, f32[128,128]{1,0:T(8,128)S(1)}, u32[]{:S(2)}) copy-start(f32[128,128]{1,0:T(8,128)S(1)} %fusion.44) | copy-start | bytes 196612
  87.6 71.5 %copy-start.32 = (f32[128]{0:T(128)}, f32[128]{0:T(128)S(1)}, u32[]{:S(2)}) copy-start(f32[128]{0:T(128)S(1)} %fusion.81) | copy-start | bytes 1540
  91.2 11.3 %collective-permute-start.17 = (f32[6,128,128]{1,0,2:T(8,128)S(1)}, f32[6,128,128]{1,0,2:T(8,128)S(1)}, u32[]{:S(2)}, u32[]{:S(2)}) collective-permute-start(f32[6,128,128]{1,0,2:T(8,128)S(1)} %copy-done.25), channel_id=1, source_target_pairs={{4,0},{8,4},{12,8},{16,12},{20,16},{24,20},{28,24},{0,28},{5,1},{9... | collective-permute-start | bytes 1179656 | tf_op jit(solution)/shard_map/ppermute | solution.py:24
  93.1 15.2 %collective-permute-start.16 = (f32[6,128,128]{1,0,2:T(8,128)S(1)}, f32[6,128,128]{1,0,2:T(8,128)S(1)}, u32[]{:S(2)}, u32[]{:S(2)}) collective-permute-start(f32[6,128,128]{1,0,2:T(8,128)S(1)} %copy-done.24), channel_id=1, source_target_pairs={{0,4},{4,8},{8,12},{12,16},{16,20},{20,24},{24,28},{28,0},{1,5},{5... | collective-permute-start | bytes 1179656 | tf_op jit(solution)/shard_map/ppermute | solution.py:23
  94.3 26.5 %collective-permute-start.9 = (f32[6,128,128]{2,1,0:T(8,128)}, f32[6,128,128]{2,1,0:T(8,128)}, u32[]{:S(2)}, u32[]{:S(2)}) collective-permute-start(f32[6,128,128]{2,1,0:T(8,128)} %get-tuple-element.65), channel_id=1, source_target_pairs={{4,0},{8,4},{12,8},{16,12},{20,16},{24,20},{28,24},{0,28},{5,1},{9... | collective-permute-start | bytes 1179656 | tf_op jit(solution)/shard_map/ppermute | solution.py:24
  102.5 24.4 %collective-permute-start.13 = (f32[6,128,128]{2,0,1:T(8,128)}, f32[6,128,128]{2,0,1:T(8,128)}, u32[]{:S(2)}, u32[]{:S(2)}) collective-permute-start(f32[6,128,128]{2,0,1:T(8,128)} %get-tuple-element.60), channel_id=1, source_target_pairs={{4,0},{8,4},{12,8},{16,12},{20,16},{24,20},{28,24},{0,28},{5,1},{9... | collective-permute-start | bytes 1179656 | tf_op jit(solution)/shard_map/ppermute | solution.py:24
  108.3 18.7 %collective-permute-start.12 = (f32[6,128,128]{2,0,1:T(8,128)}, f32[6,128,128]{2,0,1:T(8,128)}, u32[]{:S(2)}, u32[]{:S(2)}) collective-permute-start(f32[6,128,128]{2,0,1:T(8,128)} %get-tuple-element.59), channel_id=1, source_target_pairs={{0,4},{4,8},{8,12},{12,16},{16,20},{20,24},{24,28},{28,0},{1,5},{5... | collective-permute-start | bytes 1179656 | tf_op jit(solution)/shard_map/ppermute | solution.py:23
  108.6 37.0 %collective-permute-start.7 = (f32[20,6,128]{2,1,0:T(8,128)S(1)}, f32[20,6,128]{2,1,0:T(8,128)S(1)}, u32[]{:S(2)}, u32[]{:S(2)}) collective-permute-start(f32[20,6,128]{2,1,0:T(8,128)S(1)} %get-tuple-element.51), channel_id=1, source_target_pairs={{1,0},{2,1},{3,2},{0,3},{5,4},{6,5},{7,6},{4,7},{9,8},{10,9},{11,1... | collective-permute-start | bytes 184328 | tf_op jit(solution)/shard_map/ppermute | solution.py:24
  113.3 34.3 %collective-permute-start.6 = (f32[20,6,128]{2,1,0:T(8,128)S(1)}, f32[20,6,128]{2,1,0:T(8,128)S(1)}, u32[]{:S(2)}, u32[]{:S(2)}) collective-permute-start(f32[20,6,128]{2,1,0:T(8,128)S(1)} %get-tuple-element.50), channel_id=1, source_target_pairs={{0,1},{1,2},{2,3},{3,0},{4,5},{5,6},{6,7},{7,4},{8,9},{9,10},{10,1... | collective-permute-start | bytes 184328 | tf_op jit(solution)/shard_map/ppermute | solution.py:23
  120.8 27.0 %collective-permute-start.3 = (f32[20,6,128]{2,1,0:T(8,128)S(1)}, f32[20,6,128]{2,1,0:T(8,128)S(1)}, u32[]{:S(2)}, u32[]{:S(2)}) collective-permute-start(f32[20,6,128]{2,1,0:T(8,128)S(1)} %get-tuple-element.47), channel_id=1, source_target_pairs={{1,0},{2,1},{3,2},{0,3},{5,4},{6,5},{7,6},{4,7},{9,8},{10,9},{11,1... | collective-permute-start | bytes 184328 | tf_op jit(solution)/shard_map/ppermute | solution.py:24
  126.9 8.0 %collective-permute-start.19 = (f32[20,6,128]{2,0,1:T(8,128)S(1)}, f32[20,6,128]{2,0,1:T(8,128)S(1)}, u32[]{:S(2)}, u32[]{:S(2)}) collective-permute-start(f32[20,6,128]{2,0,1:T(8,128)S(1)} %copy.56), channel_id=1, source_target_pairs={{1,0},{2,1},{3,2},{0,3},{5,4},{6,5},{7,6},{4,7},{9,8},{10,9},{11,1... | collective-permute-start | bytes 184328 | tf_op jit(solution)/shard_map/ppermute | solution.py:24
  127.0 10.1 %collective-permute-start.18 = (f32[20,6,128]{2,0,1:T(8,128)S(1)}, f32[20,6,128]{2,0,1:T(8,128)S(1)}, u32[]{:S(2)}, u32[]{:S(2)}) collective-permute-start(f32[20,6,128]{2,0,1:T(8,128)S(1)} %copy.55), channel_id=1, source_target_pairs={{0,1},{1,2},{2,3},{3,0},{4,5},{5,6},{6,7},{7,4},{8,9},{9,10},{10,1... | collective-permute-start | bytes 184328 | tf_op jit(solution)/shard_map/ppermute | solution.py:23
  134.9 4.8 %collective-permute-start.15 = (f32[20,6,128]{2,0,1:T(8,128)S(1)}, f32[20,6,128]{2,0,1:T(8,128)S(1)}, u32[]{:S(2)}, u32[]{:S(2)}) collective-permute-start(f32[20,6,128]{2,0,1:T(8,128)S(1)} %get-tuple-element.41), channel_id=1, source_target_pairs={{1,0},{2,1},{3,2},{0,3},{5,4},{6,5},{7,6},{4,7},{9,8},{10,9},{11,1... | collective-permute-start | bytes 184328 | tf_op jit(solution)/shard_map/ppermute | solution.py:24
  137.1 7.1 %collective-permute-start.14 = (f32[20,6,128]{2,0,1:T(8,128)S(1)}, f32[20,6,128]{2,0,1:T(8,128)S(1)}, u32[]{:S(2)}, u32[]{:S(2)}) collective-permute-start(f32[20,6,128]{2,0,1:T(8,128)S(1)} %get-tuple-element.40), channel_id=1, source_target_pairs={{0,1},{1,2},{2,3},{3,0},{4,5},{5,6},{6,7},{7,4},{8,9},{9,10},{10,1... | collective-permute-start | bytes 184328 | tf_op jit(solution)/shard_map/ppermute | solution.py:23
  139.7 8.1 %collective-permute-start.2 = (f32[20,6,128]{2,1,0:T(8,128)S(1)}, f32[20,6,128]{2,1,0:T(8,128)S(1)}, u32[]{:S(2)}, u32[]{:S(2)}) collective-permute-start(f32[20,6,128]{2,1,0:T(8,128)S(1)} %get-tuple-element.46), channel_id=1, source_target_pairs={{0,1},{1,2},{2,3},{3,0},{4,5},{5,6},{6,7},{7,4},{8,9},{9,10},{10,1... | collective-permute-start | bytes 184328 | tf_op jit(solution)/shard_map/ppermute | solution.py:23
  144.2 4.9 %collective-permute-start.11 = (f32[20,6,128]{2,1,0:T(8,128)S(1)}, f32[20,6,128]{2,1,0:T(8,128)S(1)}, u32[]{:S(2)}, u32[]{:S(2)}) collective-permute-start(f32[20,6,128]{2,1,0:T(8,128)S(1)} %get-tuple-element.49), channel_id=1, source_target_pairs={{1,0},{2,1},{3,2},{0,3},{5,4},{6,5},{7,6},{4,7},{9,8},{10,9},{11,1... | collective-permute-start | bytes 184328 | tf_op jit(solution)/shard_map/ppermute | solution.py:24
  145.6 6.3 %collective-permute-start.10 = (f32[20,6,128]{2,1,0:T(8,128)S(1)}, f32[20,6,128]{2,1,0:T(8,128)S(1)}, u32[]{:S(2)}, u32[]{:S(2)}) collective-permute-start(f32[20,6,128]{2,1,0:T(8,128)S(1)} %get-tuple-element.48), channel_id=1, source_target_pairs={{0,1},{1,2},{2,3},{3,0},{4,5},{5,6},{6,7},{7,4},{8,9},{9,10},{10,1... | collective-permute-start | bytes 184328 | tf_op jit(solution)/shard_map/ppermute | solution.py:23
  (32 other events, 254.9 us)
where the time goes:
time: 180 us; the launch traced here: 179 us
  blocking collectives  44.2 us (25%)
  local copies, waits for them, and re-layouts  39.7 us (22%)
  other arithmetic  39.6 us (22%)
  starting transfers between devices  24.3 us (14%)
  waiting for transfers between devices  18.4 us (10%)
  matrix products  11.8 us (7%)
    psum x1, blocking collectives, level_means(): lax.psum((jnp.sum(percent, axis=(0, 1)), jnp.sum(theta_out, axis=(0, 1)))...  44.2 us
    ppermute x10, starting transfers between devices, padded_2(): after = lax.ppermute(initial, axis, down)  19.1 us
    another operation x3, other arithmetic, column_tables(): factor = jnp.linalg.cholesky(matrix)  12.4 us
    unnamed x84, local copies, waits for them, and re-layouts  11.7 us
    another operation x2, other arithmetic, column_tables(): lax.linalg.triangular_solve(factor, halfway, left_side=True, lower=True,...  10.5 us
    ppermute x10, waiting for transfers between devices, padded_2(): before = lax.ppermute(last, axis, up)  10.3 us
    ppermute x10, waiting for transfers between devices, padded_2(): after = lax.ppermute(initial, axis, down)  8.11 us
    concatenate x5, local copies, waits for them, and re-layouts, padded_2(): value = jnp.concatenate([before, value, after], axis=dim)  7.08 us
  transfers between devices with their start and end apart: 20, of which 6 were waited for; matrix products, arithmetic and copies ran while one was open for 32% of the time, Pallas kernels for 0%

commit v1 on v0

--- a/solution.py
+++ b/solution.py
@@ -111,7 +111,7 @@
 
 def level_means(percent, theta_out, columns):
     totals = lax.psum(
-        (jnp.sum(percent, axis=(0, 1)), jnp.sum(theta_out, axis=(0, 1))), ("gx", "gy")
+        lax.psum((jnp.sum(percent, axis=(0, 1)), jnp.sum(theta_out, axis=(0, 1))), "gy"), "gx"
     )
     return (totals[0] / columns, totals[1] / columns)
 

time: 180 us -> 158 us (0.88)
  blocking collectives: 44.2 us -> 24.9 us
  starting transfers between devices: 24.3 us -> 21.9 us
    psum x1, blocking collectives: 44.2 us -> 12.7 us  [level_means(): lax.psum((jnp.sum(percent, axis=(0, 1)), jnp.sum(theta_out, axis=(0, 1)))...]
    psum x0 -> x1, blocking collectives: none -> 12.2 us  [level_means(): lax.psum(lax.psum((jnp.sum(percent, axis=(0, 1)), jnp.sum(theta_out, axis...]
    ppermute x10, starting transfers between devices: 19.1 us -> 14.6 us  [padded_2(): after = lax.ppermute(initial, axis, down)]
    ppermute x10, starting transfers between devices: 5.2 us -> 7.3 us  [padded_2(): before = lax.ppermute(last, axis, up)]
  transfers between devices with their start and end apart: 20 -> 20, of which waited for: 6 -> 6; matrix products, arithmetic and copies ran while one was open for 32% -> 37% of each run, Pallas kernels for 0% -> 0%
where the time goes in v1:
time: 158 us; the launch traced here: 157 us
  other arithmetic  39.6 us (25%)
  local copies, waits for them, and re-layouts  39.5 us (25%)
  blocking collectives  24.9 us (16%)
  starting transfers between devices  21.9 us (14%)
  waiting for transfers between devices  18.2 us (12%)
  matrix products  11.8 us (7%)
    ppermute x10, starting transfers between devices, padded_2(): after = lax.ppermute(initial, axis, down)  14.6 us
    psum x1, blocking collectives, level_means(): lax.psum((jnp.sum(percent, axis=(0, 1)), jnp.sum(theta_out, axis=(0, 1)))...  12.7 us
    another operation x3, other arithmetic, column_tables(): factor = jnp.linalg.cholesky(matrix)  12.4 us
    psum x1, blocking collectives, level_means(): lax.psum(lax.psum((jnp.sum(percent, axis=(0, 1)), jnp.sum(theta_out, axis...  12.2 us
    unnamed x84, local copies, waits for them, and re-layouts  11.6 us
    another operation x2, other arithmetic, column_tables(): lax.linalg.triangular_solve(factor, halfway, left_side=True, lower=True,...  10.5 us
    ppermute x10, waiting for transfers between devices, padded_2(): before = lax.ppermute(last, axis, up)  10 us
    ppermute x10, waiting for transfers between devices, padded_2(): after = lax.ppermute(initial, axis, down)  8.22 us
  transfers between devices with their start and end apart: 20, of which 6 were waited for; matrix products, arithmetic and copies ran while one was open for 37% of the time, Pallas kernels for 0%

profile of v1, /device:TPU:0, one launch (start us, length us, event | category | flops | bytes accessed | tf_op | source)
XLA Modules:
  0.0 157.4 jit_solution(10110719615626195086)
XLA Ops:
  0.7 2.1 %fusion.102 = (f32[6,128,128]{2,1,0:T(8,128)}, f32[6,128,128]{2,1,0:T(8,128)}) fusion(f32[8,128,128]{2,1,0:T(8,128)} %param.13), kind=kLoop, calls=%fused_computation.159 | loop fusion | bytes 1572864 | tf_op jit(solution)/shard_map/slice | solution.py:22
  3.3 2.9 %collective-permute-start.5 = (f32[6,128,128]{2,1,0:T(8,128)}, f32[6,128,128]{2,1,0:T(8,128)}, u32[]{:S(2)}, u32[]{:S(2)}) collective-permute-start(f32[6,128,128]{2,1,0:T(8,128)} %get-tuple-element.69), channel_id=1, source_target_pairs={{4,0},{8,4},{12,8},{16,12},{20,16},{24,20},{28,24},{0,28},{5,1},{9... | collective-permute-start | bytes 1179656 | tf_op jit(solution)/shard_map/ppermute | solution.py:24
  7.2 2.6 %collective-permute-start.1 = (f32[6,128,128]{2,1,0:T(8,128)}, f32[6,128,128]{2,1,0:T(8,128)}, u32[]{:S(2)}, u32[]{:S(2)}) collective-permute-start(f32[6,128,128]{2,1,0:T(8,128)} %get-tuple-element.65), channel_id=1, source_target_pairs={{4,0},{8,4},{12,8},{16,12},{20,16},{24,20},{28,24},{0,28},{5,1},{9... | collective-permute-start | bytes 1179656 | tf_op jit(solution)/shard_map/ppermute | solution.py:24
  11.5 4.9 %fusion.6 = (f32[64,8,8,128]{3,2,1,0:T(8,128)}, f32[8,8,128]{2,1,0:T(8,128)S(1)}) fusion(f32[64,8,8,128]{3,2,1,0:T(8,128)} %param.17, f32[8,8,128]{2,1,0:T(8,128)S(1)} %fusion.58, s32[8,8,128]{2,1,0:T(8,128)S(1)} %copy-done.26, bf16[64,8,8,128]{3,2,1,0:T(8,128)(2,1)} %param.18), kind=kLoop, calls=%fused_computation.13 | loop fusion | flops 5758976 | bytes 5341184 | tf_op jit(solution)/shard_map/jit(_where)/select_n | solution.py:107
  17.4 12.7 %all-reduce.2 = (f32[128]{0:T(128)S(1)}, f32[128]{0:T(128)S(1)}) all-reduce(f32[128]{0:T(128)S(1)} %get-tuple-element.33, f32[128]{0:T(128)S(1)} %get-tuple-element.32), channel_id=1, replica_groups=mesh['gx'=8,'gy'=4] {'gy'}, use_global_device_ids=true, to_apply=%region_2.3 | all-reduce | flops 256 | bytes 2048 | tf_op jit(solution)/shard_map/psum | solution.py:114
  30.2 12.2 %all-reduce.1 = (f32[128]{0:T(128)S(1)}, f32[128]{0:T(128)S(1)}) all-reduce(f32[128]{0:T(128)S(1)} %get-tuple-element.36, f32[128]{0:T(128)S(1)} %get-tuple-element.37), channel_id=1, replica_groups=mesh['gx'=8,'gy'=4] {'gx'}, use_global_device_ids=true, to_apply=%region_3.4 | all-reduce | flops 256 | bytes 2048 | tf_op jit(solution)/shard_map/psum | solution.py:113
  44.6 11.7 %cholesky.17 = f32[128,128]{1,0:T(8,128)S(1)} custom-call(f32[128,128]{1,0:T(8,128)S(1)} %fusion.42), custom_call_target="Cholesky" | custom-call | tf_op jit(solution)/shard_map/jit(cholesky)/cholesky | solution.py:43
  57.6 9.8 %custom-call.8 = f32[1,128,128]{1,2,0:T(8,128)S(1)} custom-call(f32[1,128,128]{2,1,0:T(8,128)S(1)} %fusion.36), custom_call_target="InvertDiagBlocksLowerTriangular" | custom-call | tf_op jit(solution)/shard_map/triangular_solve | solution.py:46
  74.7 2.2 %collective-permute-start.9 = (f32[6,128,128]{2,1,0:T(8,128)}, f32[6,128,128]{2,1,0:T(8,128)}, u32[]{:S(2)}, u32[]{:S(2)}) collective-permute-start(f32[6,128,128]{2,1,0:T(8,128)} %get-tuple-element.67), channel_id=1, source_target_pairs={{4,0},{8,4},{12,8},{16,12},{20,16},{24,20},{28,24},{0,28},{5,1},{9... | collective-permute-start | bytes 1179656 | tf_op jit(solution)/shard_map/ppermute | solution.py:24
  78.0 4.7 %collective-permute-done.17 = f32[6,128,128]{1,0,2:T(8,128)S(1)} collective-permute-done((f32[6,128,128]{1,0,2:T(8,128)S(1)}, f32[6,128,128]{1,0,2:T(8,128)S(1)}, u32[]{:S(2)}, u32[]{:S(2)}) %collective-permute-start.17) | collective-permute-done | bytes 393248 | tf_op jit(solution)/shard_map/ppermute | solution.py:24
  82.7 2.8 %collective-permute-start.13 = (f32[6,128,128]{2,0,1:T(8,128)}, f32[6,128,128]{2,0,1:T(8,128)}, u32[]{:S(2)}, u32[]{:S(2)}) collective-permute-start(f32[6,128,128]{2,0,1:T(8,128)} %get-tuple-element.62), channel_id=1, source_target_pairs={{4,0},{8,4},{12,8},{16,12},{20,16},{24,20},{28,24},{0,28},{5,1},{9... | collective-permute-start | bytes 1179656 | tf_op jit(solution)/shard_map/ppermute | solution.py:24
  85.5 2.7 %collective-permute-done.16 = f32[6,128,128]{1,0,2:T(8,128)S(1)} collective-permute-done((f32[6,128,128]{1,0,2:T(8,128)S(1)}, f32[6,128,128]{1,0,2:T(8,128)S(1)}, u32[]{:S(2)}, u32[]{:S(2)}) %collective-permute-start.16) | collective-permute-done | bytes 393248 | tf_op jit(solution)/shard_map/ppermute | solution.py:23
  89.6 2.1 %fusion.94 = (f32[20,6,128]{1,0,2:T(8,128)}, f32[20,6,128]{1,0,2:T(8,128)}) fusion(f32[20,128,128]{1,0,2:T(8,128)S(1)} %pad_maximum_fusion.1), kind=kLoop, calls=%fused_computation.151 | loop fusion | bytes 245760 | tf_op jit(solution)/shard_map/slice | solution.py:21
  91.8 2.0 %collective-permute-start.6 = (f32[20,6,128]{2,1,0:T(8,128)S(1)}, f32[20,6,128]{2,1,0:T(8,128)S(1)}, u32[]{:S(2)}, u32[]{:S(2)}) collective-permute-start(f32[20,6,128]{2,1,0:T(8,128)S(1)} %get-tuple-element.52), channel_id=1, source_target_pairs={{0,1},{1,2},{2,3},{3,0},{4,5},{5,6},{6,7},{7,4},{8,9},{9,10},{10,1... | collective-permute-start | bytes 184328 | tf_op jit(solution)/shard_map/ppermute | solution.py:23
  105.4 2.0 %collective-permute-start.18 = (f32[20,6,128]{2,0,1:T(8,128)S(1)}, f32[20,6,128]{2,0,1:T(8,128)S(1)}, u32[]{:S(2)}, u32[]{:S(2)}) collective-permute-start(f32[20,6,128]{2,0,1:T(8,128)S(1)} %copy.55), channel_id=1, source_target_pairs={{0,1},{1,2},{2,3},{3,0},{4,5},{5,6},{6,7},{7,4},{8,9},{9,10},{10,1... | collective-permute-start | bytes 184328 | tf_op jit(solution)/shard_map/ppermute | solution.py:23
  115.7 2.2 %collective-permute-done.15 = f32[20,6,128]{2,0,1:T(8,128)S(1)} collective-permute-done((f32[20,6,128]{2,0,1:T(8,128)S(1)}, f32[20,6,128]{2,0,1:T(8,128)S(1)}, u32[]{:S(2)}, u32[]{:S(2)}) %collective-permute-start.15) | collective-permute-done | bytes 61472 | tf_op jit(solution)/shard_map/ppermute | solution.py:24
  118.0 4.5 %collective-permute-done.14 = f32[20,6,128]{2,0,1:T(8,128)S(1)} collective-permute-done((f32[20,6,128]{2,0,1:T(8,128)S(1)}, f32[20,6,128]{2,0,1:T(8,128)S(1)}, u32[]{:S(2)}, u32[]{:S(2)}) %collective-permute-start.14) | collective-permute-done | bytes 61472 | tf_op jit(solution)/shard_map/ppermute | solution.py:23
  123.8 2.1 %collective-permute-start.10 = (f32[20,6,128]{2,1,0:T(8,128)S(1)}, f32[20,6,128]{2,1,0:T(8,128)S(1)}, u32[]{:S(2)}, u32[]{:S(2)}) collective-permute-start(f32[20,6,128]{2,1,0:T(8,128)S(1)} %get-tuple-element.50), channel_id=1, source_target_pairs={{0,1},{1,2},{2,3},{3,0},{4,5},{5,6},{6,7},{7,4},{8,9},{9,10},{10,1... | collective-permute-start | bytes 184328 | tf_op jit(solution)/shard_map/ppermute | solution.py:23
  127.3 2.8 %collective-permute-done.10 = f32[20,6,128]{2,1,0:T(8,128)S(1)} collective-permute-done((f32[20,6,128]{2,1,0:T(8,128)S(1)}, f32[20,6,128]{2,1,0:T(8,128)S(1)}, u32[]{:S(2)}, u32[]{:S(2)}) %collective-permute-start.10) | collective-permute-done | bytes 61472 | tf_op jit(solution)/shard_map/ppermute | solution.py:23
  135.2 2.1 %reshape.77 = f32[1584,128]{1,0:T(8,128)} reshape(f32[12,132,128]{2,1,0:T(8,128)} %fusion.23) | data formatting | bytes 1622016 | tf_op jit(solution)/shard_map/reshape | solution.py:61
  137.3 2.3 %fusion.21 = f32[12,132,128]{2,1,0:T(8,128)} fusion(f32[20,140,128]{2,1,0:T(8,128)} %copy-done.2, f32[16,136,128]{2,1,0:T(8,128)S(1)} %bitcast.50, f32[128]{0:T(128)S(1)} %fusion.81), kind=kLoop, calls=%fused_computation.50 | loop fusion | flops 608256 | bytes 2433536 | tf_op jit(solution)/shard_map/mul | solution.py:60
  139.5 2.2 %reshape.79 = f32[1584,128]{1,0:T(8,128)} reshape(f32[12,132,128]{2,1,0:T(8,128)} %fusion.21) | data formatting | bytes 1622016 | tf_op jit(solution)/shard_map/reshape | solution.py:60
  141.7 1.9 %fusion.104 = f32[1584,128]{1,0:T(8,128)S(1)} fusion(f32[1584,128]{1,0:T(8,128)} %reshape.79, f32[128,128]{1,0:T(8,128)S(1)} %fusion.37), kind=kOutput, calls=%fused_computation.161 | convolution fusion | flops 311427072 | bytes 1687552 | tf_op jit(solution)/shard_map/dot_general | solution.py:62
  147.2 2.1 %reshape.81 = f32[12,132,128]{2,1,0:T(8,128)} reshape(f32[1584,128]{1,0:T(8,128)} %copy-done.5) | data formatting | bytes 1622016 | tf_op jit(solution)/shard_map/reshape | solution.py:72
  (171 shorter events, 56.4 us)
Async XLA Ops:
  2.8 69.0 %collective-permute-start.4 = (f32[6,128,128]{2,1,0:T(8,128)}, f32[6,128,128]{2,1,0:T(8,128)}, u32[]{:S(2)}, u32[]{:S(2)}) collective-permute-start(f32[6,128,128]{2,1,0:T(8,128)} %get-tuple-element.70), channel_id=1, source_target_pairs={{0,4},{4,8},{8,12},{12,16},{16,20},{20,24},{24,28},{28,0},{1,5},{5... | collective-permute-start | bytes 1179656 | tf_op jit(solution)/shard_map/ppermute | solution.py:23
  3.3 71.4 %collective-permute-start.5 = (f32[6,128,128]{2,1,0:T(8,128)}, f32[6,128,128]{2,1,0:T(8,128)}, u32[]{:S(2)}, u32[]{:S(2)}) collective-permute-start(f32[6,128,128]{2,1,0:T(8,128)} %get-tuple-element.69), channel_id=1, source_target_pairs={{4,0},{8,4},{12,8},{16,12},{20,16},{24,20},{28,24},{0,28},{5,1},{9... | collective-permute-start | bytes 1179656 | tf_op jit(solution)/shard_map/ppermute | solution.py:24
  7.2 65.9 %collective-permute-start = (f32[6,128,128]{2,1,0:T(8,128)}, f32[6,128,128]{2,1,0:T(8,128)}, u32[]{:S(2)}, u32[]{:S(2)}) collective-permute-start(f32[6,128,128]{2,1,0:T(8,128)} %get-tuple-element.66), channel_id=1, source_target_pairs={{0,4},{4,8},{8,12},{12,16},{16,20},{20,24},{24,28},{28,0},{1,5},{5... | collective-permute-start | bytes 1179656 | tf_op jit(solution)/shard_map/ppermute | solution.py:23
  7.2 84.6 %collective-permute-start.1 = (f32[6,128,128]{2,1,0:T(8,128)}, f32[6,128,128]{2,1,0:T(8,128)}, u32[]{:S(2)}, u32[]{:S(2)}) collective-permute-start(f32[6,128,128]{2,1,0:T(8,128)} %get-tuple-element.65), channel_id=1, source_target_pairs={{4,0},{8,4},{12,8},{16,12},{20,16},{24,20},{28,24},{0,28},{5,1},{9... | collective-permute-start | bytes 1179656 | tf_op jit(solution)/shard_map/ppermute | solution.py:24
  10.8 77.7 %collective-permute-start.8 = (f32[6,128,128]{2,1,0:T(8,128)}, f32[6,128,128]{2,1,0:T(8,128)}, u32[]{:S(2)}, u32[]{:S(2)}) collective-permute-start(f32[6,128,128]{2,1,0:T(8,128)} %get-tuple-element.68), channel_id=1, source_target_pairs={{0,4},{4,8},{8,12},{12,16},{16,20},{20,24},{24,28},{28,0},{1,5},{5... | collective-permute-start | bytes 1179656 | tf_op jit(solution)/shard_map/ppermute | solution.py:23
  10.8 133.7 %copy-start.28 = (s32[128]{0:T(128)}, s32[128]{0:T(128)S(1)}, u32[]{:S(2)}) copy-start(s32[128]{0:T(128)S(1)} %iota_add_fusion) | copy-start | bytes 1540
  10.8 133.7 %copy-start.30 = (pred[128]{0:T(512)(128)(4,1)}, pred[128]{0:T(512)(128)(4,1)S(1)}, u32[]{:S(2)}) copy-start(pred[128]{0:T(512)(128)(4,1)S(1)} %iota_compare_fusion.6) | copy-start | bytes 388
  68.3 75.4 %copy-start.19 = (f32[128,128]{1,0:T(8,128)}, f32[128,128]{1,0:T(8,128)S(1)}, u32[]{:S(2)}) copy-start(f32[128,128]{1,0:T(8,128)S(1)} %fusion.44) | copy-start | bytes 196612
  68.3 68.9 %copy-start.32 = (f32[128]{0:T(128)}, f32[128]{0:T(128)S(1)}, u32[]{:S(2)}) copy-start(f32[128]{0:T(128)S(1)} %fusion.81) | copy-start | bytes 1540
  71.9 10.8 %collective-permute-start.17 = (f32[6,128,128]{1,0,2:T(8,128)S(1)}, f32[6,128,128]{1,0,2:T(8,128)S(1)}, u32[]{:S(2)}, u32[]{:S(2)}) collective-permute-start(f32[6,128,128]{1,0,2:T(8,128)S(1)} %copy-done.25), channel_id=1, source_target_pairs={{4,0},{8,4},{12,8},{16,12},{20,16},{24,20},{28,24},{0,28},{5,1},{9... | collective-permute-start | bytes 1179656 | tf_op jit(solution)/shard_map/ppermute | solution.py:24
  73.1 15.2 %collective-permute-start.16 = (f32[6,128,128]{1,0,2:T(8,128)S(1)}, f32[6,128,128]{1,0,2:T(8,128)S(1)}, u32[]{:S(2)}, u32[]{:S(2)}) collective-permute-start(f32[6,128,128]{1,0,2:T(8,128)S(1)} %copy-done.24), channel_id=1, source_target_pairs={{0,4},{4,8},{8,12},{12,16},{16,20},{20,24},{24,28},{28,0},{1,5},{5... | collective-permute-start | bytes 1179656 | tf_op jit(solution)/shard_map/ppermute | solution.py:23
  74.7 26.0 %collective-permute-start.9 = (f32[6,128,128]{2,1,0:T(8,128)}, f32[6,128,128]{2,1,0:T(8,128)}, u32[]{:S(2)}, u32[]{:S(2)}) collective-permute-start(f32[6,128,128]{2,1,0:T(8,128)} %get-tuple-element.67), channel_id=1, source_target_pairs={{4,0},{8,4},{12,8},{16,12},{20,16},{24,20},{28,24},{0,28},{5,1},{9... | collective-permute-start | bytes 1179656 | tf_op jit(solution)/shard_map/ppermute | solution.py:24
  82.7 22.6 %collective-permute-start.13 = (f32[6,128,128]{2,0,1:T(8,128)}, f32[6,128,128]{2,0,1:T(8,128)}, u32[]{:S(2)}, u32[]{:S(2)}) collective-permute-start(f32[6,128,128]{2,0,1:T(8,128)} %get-tuple-element.62), channel_id=1, source_target_pairs={{4,0},{8,4},{12,8},{16,12},{20,16},{24,20},{28,24},{0,28},{5,1},{9... | collective-permute-start | bytes 1179656 | tf_op jit(solution)/shard_map/ppermute | solution.py:24
  88.2 17.2 %collective-permute-start.12 = (f32[6,128,128]{2,0,1:T(8,128)}, f32[6,128,128]{2,0,1:T(8,128)}, u32[]{:S(2)}, u32[]{:S(2)}) collective-permute-start(f32[6,128,128]{2,0,1:T(8,128)} %get-tuple-element.61), channel_id=1, source_target_pairs={{0,4},{4,8},{8,12},{12,16},{16,20},{20,24},{24,28},{28,0},{1,5},{5... | collective-permute-start | bytes 1179656 | tf_op jit(solution)/shard_map/ppermute | solution.py:23
  88.5 35.3 %collective-permute-start.7 = (f32[20,6,128]{2,1,0:T(8,128)S(1)}, f32[20,6,128]{2,1,0:T(8,128)S(1)}, u32[]{:S(2)}, u32[]{:S(2)}) collective-permute-start(f32[20,6,128]{2,1,0:T(8,128)S(1)} %get-tuple-element.53), channel_id=1, source_target_pairs={{1,0},{2,1},{3,2},{0,3},{5,4},{6,5},{7,6},{4,7},{9,8},{10,9},{11,1... | collective-permute-start | bytes 184328 | tf_op jit(solution)/shard_map/ppermute | solution.py:24
  91.8 34.1 %collective-permute-start.6 = (f32[20,6,128]{2,1,0:T(8,128)S(1)}, f32[20,6,128]{2,1,0:T(8,128)S(1)}, u32[]{:S(2)}, u32[]{:S(2)}) collective-permute-start(f32[20,6,128]{2,1,0:T(8,128)S(1)} %get-tuple-element.52), channel_id=1, source_target_pairs={{0,1},{1,2},{2,3},{3,0},{4,5},{5,6},{6,7},{7,4},{8,9},{9,10},{10,1... | collective-permute-start | bytes 184328 | tf_op jit(solution)/shard_map/ppermute | solution.py:23
  100.7 25.3 %collective-permute-start.3 = (f32[20,6,128]{2,1,0:T(8,128)S(1)}, f32[20,6,128]{2,1,0:T(8,128)S(1)}, u32[]{:S(2)}, u32[]{:S(2)}) collective-permute-start(f32[20,6,128]{2,1,0:T(8,128)S(1)} %get-tuple-element.49), channel_id=1, source_target_pairs={{1,0},{2,1},{3,2},{0,3},{5,4},{6,5},{7,6},{4,7},{9,8},{10,9},{11,1... | collective-permute-start | bytes 184328 | tf_op jit(solution)/shard_map/ppermute | solution.py:24
  105.4 8.0 %collective-permute-start.19 = (f32[20,6,128]{2,0,1:T(8,128)S(1)}, f32[20,6,128]{2,0,1:T(8,128)S(1)}, u32[]{:S(2)}, u32[]{:S(2)}) collective-permute-start(f32[20,6,128]{2,0,1:T(8,128)S(1)} %copy.56), channel_id=1, source_target_pairs={{1,0},{2,1},{3,2},{0,3},{5,4},{6,5},{7,6},{4,7},{9,8},{10,9},{11,1... | collective-permute-start | bytes 184328 | tf_op jit(solution)/shard_map/ppermute | solution.py:24
  105.4 9.9 %collective-permute-start.18 = (f32[20,6,128]{2,0,1:T(8,128)S(1)}, f32[20,6,128]{2,0,1:T(8,128)S(1)}, u32[]{:S(2)}, u32[]{:S(2)}) collective-permute-start(f32[20,6,128]{2,0,1:T(8,128)S(1)} %copy.55), channel_id=1, source_target_pairs={{0,1},{1,2},{2,3},{3,0},{4,5},{5,6},{6,7},{7,4},{8,9},{9,10},{10,1... | collective-permute-start | bytes 184328 | tf_op jit(solution)/shard_map/ppermute | solution.py:23
  113.3 4.6 %collective-permute-start.15 = (f32[20,6,128]{2,0,1:T(8,128)S(1)}, f32[20,6,128]{2,0,1:T(8,128)S(1)}, u32[]{:S(2)}, u32[]{:S(2)}) collective-permute-start(f32[20,6,128]{2,0,1:T(8,128)S(1)} %get-tuple-element.43), channel_id=1, source_target_pairs={{1,0},{2,1},{3,2},{0,3},{5,4},{6,5},{7,6},{4,7},{9,8},{10,9},{11,1... | collective-permute-start | bytes 184328 | tf_op jit(solution)/shard_map/ppermute | solution.py:24
  115.3 7.1 %collective-permute-start.14 = (f32[20,6,128]{2,0,1:T(8,128)S(1)}, f32[20,6,128]{2,0,1:T(8,128)S(1)}, u32[]{:S(2)}, u32[]{:S(2)}) collective-permute-start(f32[20,6,128]{2,0,1:T(8,128)S(1)} %get-tuple-element.42), channel_id=1, source_target_pairs={{0,1},{1,2},{2,3},{3,0},{4,5},{5,6},{6,7},{7,4},{8,9},{9,10},{10,1... | collective-permute-start | bytes 184328 | tf_op jit(solution)/shard_map/ppermute | solution.py:23
  117.9 8.1 %collective-permute-start.2 = (f32[20,6,128]{2,1,0:T(8,128)S(1)}, f32[20,6,128]{2,1,0:T(8,128)S(1)}, u32[]{:S(2)}, u32[]{:S(2)}) collective-permute-start(f32[20,6,128]{2,1,0:T(8,128)S(1)} %get-tuple-element.48), channel_id=1, source_target_pairs={{0,1},{1,2},{2,3},{3,0},{4,5},{5,6},{6,7},{7,4},{8,9},{9,10},{10,1... | collective-permute-start | bytes 184328 | tf_op jit(solution)/shard_map/ppermute | solution.py:23
  122.4 4.8 %collective-permute-start.11 = (f32[20,6,128]{2,1,0:T(8,128)S(1)}, f32[20,6,128]{2,1,0:T(8,128)S(1)}, u32[]{:S(2)}, u32[]{:S(2)}) collective-permute-start(f32[20,6,128]{2,1,0:T(8,128)S(1)} %get-tuple-element.51), channel_id=1, source_target_pairs={{1,0},{2,1},{3,2},{0,3},{5,4},{6,5},{7,6},{4,7},{9,8},{10,9},{11,1... | collective-permute-start | bytes 184328 | tf_op jit(solution)/shard_map/ppermute | solution.py:24
  123.8 6.3 %collective-permute-start.10 = (f32[20,6,128]{2,1,0:T(8,128)S(1)}, f32[20,6,128]{2,1,0:T(8,128)S(1)}, u32[]{:S(2)}, u32[]{:S(2)}) collective-permute-start(f32[20,6,128]{2,1,0:T(8,128)S(1)} %get-tuple-element.50), channel_id=1, source_target_pairs={{0,1},{1,2},{2,3},{3,0},{4,5},{5,6},{6,7},{7,4},{8,9},{9,10},{10,1... | collective-permute-start | bytes 184328 | tf_op jit(solution)/shard_map/ppermute | solution.py:23
  (32 other events, 231.7 us)
